TPU v7x, 32 devices: a whole 2x2x4 slice. The times are simulated.
32 devices in a mesh: dev: 32 (over z, y, x, core).
Axes of the slice: x: 2, y: 2, z: 4, core: 2. Of those that a mesh axis runs over, the one named last changes fastest.
Arguments:
- state: float32 [128, 512, 128], P('dev'), may hold values from -6 to 6
- background: float32 [128, 512, 128], P('dev'), may hold values from -6 to 6
- back_precision: float32 [128], replicated, may hold values from 0.2 to 2
- conv_first: bfloat16 [3, 3, 128, 128], replicated, may hold values from -0.1875 to 0.1875
- bias_first: float32 [128], replicated, may hold values from -3 to 3
- conv_second: bfloat16 [3, 3, 128, 128], replicated, may hold values from -0.1875 to 0.1875
- sounding_tile: int32 [16384, 1], P('dev'), may hold values from 0 to 31; in each aligned block of 512 rows (0 to 511, 512 to 1023, ...) at most 32 rows name the same one
- sounding_cells: int32 [16384, 4], P('dev'), may hold values from 0 to 2047
- cell_weights: float32 [16384, 4], P('dev'), may hold values from 0.1 to 1
- observations: float32 [16384, 616], P('dev'), may hold values from -6 to 6
- live_counts: int32 [32], P('dev'), may hold values from 1 to 511, as said below
- layer_in: bfloat16 [128, 1024], replicated, may hold values from -0.5 to 0.5
- bias_in: float32 [1024], replicated, may hold values from -3 to 3
- layer_out: bfloat16 [1024, 616], replicated, may hold values from -0.1875 to 0.1875
- bias_out: float32 [616], replicated, may hold values from -3 to 3
- error_precision: float32 [616, 616], replicated, as said below
Outputs:
- gradient: float32 [128, 512, 128], P('dev')
Inputs may be any that keep to these rules, and one draw needn't show every extreme that they name: `sounding_tile`: among the 512 soundings of one list, at most 32 lie in the same strip, and in some lists some strip holds exactly 32 of them. The live soundings of a list are its first live_counts; the counts of lists l and l + 16 sum to 512. `error_precision`: Symmetric.
All inputs are finite; a program needn't handle non-finite values.
Results may differ from a plain program's by a relative error of at most 0.008.
Values may be sent and summed in bfloat16 or wider, within the bound.
A program may use at most 64 MiB of HBM per device.

v0:
```python
import functools

import jax
import jax.numpy as jnp
from jax import lax
from jax.experimental import pallas as pl
from jax.experimental.pallas import tpu as pltpu
from jax.sharding import PartitionSpec as P

F32 = jnp.float32
BF16 = jnp.bfloat16
MESH = pl.DeviceIdType.MESH
LANES = 128


def dot(a, b):
    return jnp.dot(a, b, preferred_element_type=F32)


def dot_nt(a, b):
    return lax.dot_general(a, b, (((1,), (1,)), ((), ())), preferred_element_type=F32)


def kernel(
    n,
    table_ref,
    live_ref,
    back_precision_ref,
    bias_first_ref,
    bias_in_ref,
    bias_out_ref,
    state_hbm,
    background_hbm,
    conv_first_hbm,
    conv_second_hbm,
    observations_hbm,
    layer_in_hbm,
    layer_out_hbm,
    precision_hbm,
    out_ref,
    state_ref,
    background_ref,
    conv_first_ref,
    conv_second_ref,
    adj_first_ref,
    adj_second_ref,
    observations_ref,
    layer_in_ref,
    layer_out_ref,
    precision_ref,
    field_ref,
    halo_ref,
    taps_ref,
    hidden_ref,
    hidden_taps_ref,
    observed_t_ref,
    place_ref,
    place_t_ref,
    share_t_ref,
    grad_ref,
    req_src,
    req_dst,
    ret_src,
    ret_dst,
    out_src,
    out_dst,
    load_sem,
    halo_send,
    halo_recv,
    req_send,
    req_recv,
    ret_send,
    ret_recv,
    out_send,
    out_recv,
):
    me = lax.axis_index("dev")
    rows, cols, ch = state_ref.shape
    slots = place_t_ref.shape[0]
    listed = place_t_ref.shape[1]
    cap = slots // n
    per = LANES // cap
    groups = slots // LANES
    up = lax.rem(me + n - 1, n)
    down = lax.rem(me + 1, n)

    loads = [
        pltpu.make_async_copy(src, dst, load_sem.at[i])
        for i, (src, dst) in enumerate(
            (
                (state_hbm, state_ref),
                (conv_first_hbm, conv_first_ref),
                (conv_second_hbm, conv_second_ref),
                (layer_in_hbm, layer_in_ref),
                (layer_out_hbm, layer_out_ref),
                (observations_hbm, observations_ref),
                (precision_hbm, precision_ref),
                (background_hbm, background_ref),
            )
        )
    ]
    for load in loads:
        load.start()

    barrier = pltpu.get_barrier_semaphore()

    def greet(k, carry):
        pl.semaphore_signal(
            barrier, inc=1, device_id=(lax.rem(me + k, n),), device_id_type=MESH
        )
        return carry

    lax.fori_loop(1, n, greet, 0)

    def exchange(src, dst, send, recv):
        def start(k, carry):
            target = lax.rem(me + k, n)
            pltpu.make_async_remote_copy(
                src_ref=src.at[target],
                dst_ref=dst.at[me],
                send_sem=send.at[k],
                recv_sem=recv.at[k],
                device_id=(target,),
                device_id_type=MESH,
            ).start()
            return carry

        lax.fori_loop(1, n, start, 0)

    def settle(src, dst, send, recv):
        def wait(k, carry):
            copy = pltpu.make_async_remote_copy(
                src_ref=src.at[lax.rem(me + k, n)],
                dst_ref=dst.at[lax.rem(me + n - k, n)],
                send_sem=send.at[k],
                recv_sem=recv.at[k],
                device_id=(lax.rem(me + k, n),),
                device_id_type=MESH,
            )
            copy.wait_recv()
            copy.wait_send()
            return carry

        lax.fori_loop(1, n, wait, 0)

    def rim(phase):
        return [
            pltpu.make_async_remote_copy(
                src_ref=field_ref.at[phase, pl.ds(rows - 2 if side == 0 else 0, 2)],
                dst_ref=halo_ref.at[phase, side],
                send_sem=halo_send.at[phase, side],
                recv_sem=halo_recv.at[phase, side],
                device_id=(down if side == 0 else up,),
                device_id_type=MESH,
            )
            for side in range(2)
        ]

    def put_taps(taps, row, value):
        taps[row, :, pl.ds(0, ch)] = pltpu.roll(value, 1, 0).astype(BF16)
        taps[row, :, pl.ds(ch, ch)] = value.astype(BF16)
        taps[row, :, pl.ds(2 * ch, ch)] = pltpu.roll(value, cols - 1, 0).astype(BF16)

    def conv_row(taps, row, weights):
        return (
            dot(taps[row], weights[0])
            + dot(taps[row + 1], weights[1])
            + dot(taps[row + 2], weights[2])
        )

    def put_halo(phase):
        for side in range(2):
            inside = (me > 0) if side == 0 else (me < n - 1)
            for i in range(2):
                value = halo_ref[phase, side, i].astype(F32) * inside.astype(F32)
                put_taps(taps_ref, i if side == 0 else rows + 2 + i, value)

    def within(row):
        first, last = me == 0, me == n - 1
        return 1.0 - jnp.where(
            (first & (row == 0)) | (last & (row == rows + 1)), 1.0, 0.0
        ).astype(F32)

    loads[0].wait()

    def take_state(r, carry):
        field_ref[0, r] = state_ref[r].astype(BF16)
        return carry

    lax.fori_loop(0, rows, take_state, 0)

    table = table_ref[...]
    tile_row = table[8:9]
    tile_col = jnp.broadcast_to(tile_row, (LANES, listed)).T[:, 0:1]
    same = tile_col == tile_row
    from_col = lax.broadcasted_iota(jnp.int32, (listed, listed), 0)
    from_row = lax.broadcasted_iota(jnp.int32, (listed, listed), 1)
    rank_row = jnp.sum(jnp.where(same & (from_col < from_row), 1.0, 0.0), axis=0, keepdims=True)
    rank_col = jnp.sum(jnp.where(same & (from_row < from_col), 1.0, 0.0), axis=1, keepdims=True)
    slot_row = (tile_row * cap + rank_row).astype(jnp.int32)
    slot_col = (tile_col * cap + rank_col).astype(jnp.int32)
    for g in range(groups):
        rowid = lax.broadcasted_iota(jnp.int32, (LANES, listed), 0) + g * LANES
        place_t_ref[pl.ds(g * LANES, LANES)] = jnp.where(rowid == slot_row, 1.0, 0.0).astype(BF16)
        colid = lax.broadcasted_iota(jnp.int32, (listed, LANES), 1) + g * LANES
        place_ref[:, pl.ds(g * LANES, LANES)] = jnp.where(colid == slot_col, 1.0, 0.0).astype(BF16)

    values = table[0:8]
    part_1 = values.astype(BF16).astype(F32)
    part_2 = (values - part_1).astype(BF16).astype(F32)
    part_3 = values - part_1 - part_2
    parts = jnp.concatenate([part_1, part_2, part_3, jnp.zeros_like(values)], axis=0).astype(BF16)
    own_lanes = lax.broadcasted_iota(jnp.int32, (8, LANES), 1) // cap == lax.rem(me, per)
    for g in range(groups):
        spread = dot_nt(parts, place_t_ref[pl.ds(g * LANES, LANES)])
        spread = spread[0:8] + spread[8:16] + spread[16:24]
        for i in range(per):
            turned = pltpu.roll(spread, lax.rem(lax.rem(me, per) + per - i, per) * cap, 1)
            req_src[g * per + i] = jnp.where(own_lanes, turned, 0.0)
    req_dst[me] = req_src[me]

    pl.semaphore_wait(barrier, n - 1)
    forward_rim = rim(0)
    for copy in forward_rim:
        copy.start()
    exchange(req_src, req_dst, req_send, req_recv)

    def take_taps(r, carry):
        put_taps(taps_ref, r + 2, state_ref[r].astype(BF16).astype(F32))
        return carry

    lax.fori_loop(0, rows, take_taps, 0)
    loads[1].wait()
    loads[2].wait()
    for kernel_ref, adj_ref in ((conv_first_ref, adj_first_ref), (conv_second_ref, adj_second_ref)):
        for a in range(3):
            for b in range(3):
                tap = kernel_ref[2 - a, pl.ds((2 - b) * ch, ch)].astype(F32)
                adj_ref[a, pl.ds(b * ch, ch)] = tap.T.astype(BF16)

    def forward_row(row, carry):
        value = jnp.tanh(conv_row(taps_ref, row, conv_first_ref) + bias_first_ref[...])
        value = value.astype(BF16).astype(F32) * within(row)
        hidden_ref[row] = value
        put_taps(hidden_taps_ref, row, value)
        return carry

    lax.fori_loop(2, rows, forward_row, 0)
    for copy in forward_rim:
        copy.wait_recv()
    put_halo(0)
    lax.fori_loop(0, 2, forward_row, 0)
    lax.fori_loop(rows, rows + 2, forward_row, 0)

    def observed_row(r, carry):
        value = state_ref[r] + conv_row(hidden_taps_ref, r, conv_second_ref)
        observed_t_ref[:, pl.ds(pl.multiple_of(r * cols, LANES), cols)] = value.T.astype(BF16)
        return carry

    lax.fori_loop(0, rows, observed_row, 0)

    settle(req_src, req_dst, req_send, req_recv)
    wanted = []
    for g in range(groups):
        total = req_dst[g * per]
        for i in range(1, per):
            total = total + req_dst[g * per + i]
        wanted.append(total)
    margin = 4

    def build_shares(c, carry):
        base = pl.multiple_of(c * LANES, LANES)
        cell = (lax.broadcasted_iota(jnp.int32, (LANES, LANES), 0) + base).astype(F32)
        for g in range(groups):
            total = jnp.zeros((LANES, LANES), F32)
            for k in range(margin):
                total = total + jnp.where(
                    cell == wanted[g][k : k + 1], wanted[g][margin + k : margin + k + 1], 0.0
                )
            share_t_ref[pl.ds(base, LANES), pl.ds(g * LANES, LANES)] = total.astype(BF16)
        return carry

    lax.fori_loop(0, rows * cols // LANES, build_shares, 0)

    def blend(g, carry):
        width = 2 * LANES
        base = pl.multiple_of(g * width, width)
        blended = dot(observed_t_ref[...], share_t_ref[:, pl.ds(base, width)]).T
        ret_src[pl.ds(g * (width // cap), width // cap)] = blended.reshape(
            width // cap, cap, ch
        ).astype(BF16)
        return carry

    lax.fori_loop(0, groups // 2, blend, 0)
    ret_dst[me] = ret_src[me]
    exchange(ret_src, ret_dst, ret_send, ret_recv)
    for load in loads[3:7]:
        load.wait()
    precision = precision_ref[...].astype(BF16)
    settle(ret_src, ret_dst, ret_send, ret_recv)
    returned = ret_dst[...].astype(F32).reshape(slots, ch).astype(BF16)
    live = live_ref[0]
    block = listed // 4
    for s in range(0, listed, block):
        span = pl.ds(s, block)
        interpolated = dot(place_ref[span], returned).astype(BF16)
        activated = jnp.tanh(dot(interpolated, layer_in_ref[...]) + bias_in_ref[...]).astype(BF16)
        radiance = dot(activated, layer_out_ref[...]) + bias_out_ref[...]
        alive = lax.broadcasted_iota(jnp.int32, (block, 1), 0) + s < live
        innovation = jnp.where(alive, radiance - observations_ref[span], 0.0)
        weighted = dot(innovation.astype(BF16), precision)
        back_act = dot_nt(weighted.astype(BF16), layer_out_ref[...])
        act_wide = activated.astype(F32)
        pre_grad = (back_act * (1.0 - act_wide * act_wide)).astype(BF16)
        grad_ref[span] = dot_nt(pre_grad, layer_in_ref[...]).astype(BF16)

    def dispatch(g, carry):
        width = 2 * LANES
        base = pl.multiple_of(g * width, width)
        outgoing = dot(place_t_ref[pl.ds(base, width)], grad_ref[...])
        out_src[pl.ds(g * (width // cap), width // cap)] = outgoing.reshape(
            width // cap, cap, ch
        ).astype(BF16)
        return carry

    lax.fori_loop(0, groups // 2, dispatch, 0)
    out_dst[me] = out_src[me]
    exchange(out_src, out_dst, out_send, out_recv)
    settle(out_src, out_dst, out_send, out_recv)
    arrived = out_dst[...].astype(F32).reshape(slots, ch).astype(BF16)

    def gather_grad(r, carry):
        value = dot(share_t_ref[pl.ds(pl.multiple_of(r * cols, LANES), cols)], arrived)
        out_ref[r] = value
        field_ref[1, r] = value.astype(BF16)
        return carry

    lax.fori_loop(0, rows, gather_grad, 0)
    for copy in forward_rim:
        copy.wait_send()
    backward_rim = rim(1)
    for copy in backward_rim:
        copy.start()

    def take_grad(r, carry):
        put_taps(taps_ref, r + 2, out_ref[r].astype(BF16).astype(F32))
        return carry

    lax.fori_loop(0, rows, take_grad, 0)

    def backward_row(row, carry):
        value = conv_row(taps_ref, row, adj_second_ref)
        hidden = hidden_ref[row]
        value = value * (1.0 - hidden * hidden) * within(row)
        put_taps(hidden_taps_ref, row, value.astype(BF16).astype(F32))
        return carry

    lax.fori_loop(2, rows, backward_row, 0)
    for copy in backward_rim:
        copy.wait_recv()
    put_halo(1)
    lax.fori_loop(0, 2, backward_row, 0)
    lax.fori_loop(rows, rows + 2, backward_row, 0)
    loads[7].wait()

    def last_row(r, carry):
        out_ref[r] = (
            out_ref[r]
            + conv_row(hidden_taps_ref, r, adj_first_ref)
            + back_precision_ref[...] * (state_ref[r] - background_ref[r])
        )
        return carry

    lax.fori_loop(0, rows, last_row, 0)
    for copy in backward_rim:
        copy.wait_send()


def per_device(
    state,
    background,
    back_precision,
    conv_first,
    bias_first,
    conv_second,
    sounding_tile,
    sounding_cells,
    cell_weights,
    observations,
    live_counts,
    layer_in,
    bias_in,
    layer_out,
    bias_out,
    error_precision,
):
    rows, cols, ch = state.shape
    n = lax.axis_size("dev")
    listed = sounding_tile.shape[0]
    slots = 2 * listed
    cap = slots // n
    hid, chan = layer_out.shape
    table = jnp.concatenate(
        [
            sounding_cells.T.astype(F32),
            cell_weights.T,
            jnp.broadcast_to(sounding_tile.reshape(1, listed).astype(F32), (8, listed)),
        ],
        axis=0,
    )
    vmem = pl.BlockSpec(memory_space=pltpu.VMEM)
    hbm = pl.BlockSpec(memory_space=pl.ANY)
    dma = pltpu.SemaphoreType.DMA
    return pl.pallas_call(
        functools.partial(kernel, n),
        out_shape=jax.ShapeDtypeStruct(state.shape, F32),
        in_specs=[vmem, pl.BlockSpec(memory_space=pltpu.SMEM)] + [vmem] * 4 + [hbm] * 8,
        out_specs=vmem,
        scratch_shapes=[
            pltpu.VMEM(state.shape, F32),
            pltpu.VMEM(state.shape, F32),
            pltpu.VMEM((3, 3 * ch, ch), BF16),
            pltpu.VMEM((3, 3 * ch, ch), BF16),
            pltpu.VMEM((3, 3 * ch, ch), BF16),
            pltpu.VMEM((3, 3 * ch, ch), BF16),
            pltpu.VMEM((listed, chan), F32),
            pltpu.VMEM((ch, hid), BF16),
            pltpu.VMEM((hid, chan), BF16),
            pltpu.VMEM((chan, chan), F32),
            pltpu.VMEM((2, rows, cols, ch), BF16),
            pltpu.VMEM((2, 2, 2, cols, ch), BF16),
            pltpu.VMEM((rows + 4, cols, 3 * ch), BF16),
            pltpu.VMEM((rows + 2, cols, ch), F32),
            pltpu.VMEM((rows + 2, cols, 3 * ch), BF16),
            pltpu.VMEM((ch, rows * cols), BF16),
            pltpu.VMEM((listed, slots), BF16),
            pltpu.VMEM((slots, listed), BF16),
            pltpu.VMEM((rows * cols, slots), BF16),
            pltpu.VMEM((listed, ch), BF16),
            pltpu.VMEM((n, 8, LANES), F32),
            pltpu.VMEM((n, 8, LANES), F32),
            pltpu.VMEM((n, cap, ch), BF16),
            pltpu.VMEM((n, cap, ch), BF16),
            pltpu.VMEM((n, cap, ch), BF16),
            pltpu.VMEM((n, cap, ch), BF16),
            dma((8,)),
            dma((2, 2)),
            dma((2, 2)),
            dma((n,)),
            dma((n,)),
            dma((n,)),
            dma((n,)),
            dma((n,)),
            dma((n,)),
        ],
        compiler_params=pltpu.CompilerParams(
            collective_id=0, has_side_effects=True, vmem_limit_bytes=60 * 1024 * 1024
        ),
        name="step",
    )(
        table,
        live_counts,
        back_precision.reshape(1, -1),
        bias_first.reshape(1, -1),
        bias_in.reshape(1, -1),
        bias_out.reshape(1, -1),
        state,
        background,
        conv_first.reshape(3, 3 * ch, ch),
        conv_second.reshape(3, 3 * ch, ch),
        observations,
        layer_in,
        layer_out,
        error_precision,
    )


def solution(mesh):
    return jax.shard_map(
        per_device,
        mesh=mesh,
        in_specs=(
            P("dev", None, None),
            P("dev", None, None),
            P(),
            P(),
            P(),
            P(),
            P("dev", None),
            P("dev", None),
            P("dev", None),
            P("dev", None),
            P("dev"),
            P(),
            P(),
            P(),
            P(),
            P(),
        ),
        out_specs=P("dev", None, None),
        check_vma=False,
    )
```

profile of v0, /device:TPU:0, one launch (start us, length us, event | category | flops | bytes accessed | tf_op | source)
XLA Modules:
  0.0 75.1 jit_solution(9716629148661953551)
XLA Ops:
  0.7 0.7 convert_element_type.19
  1.3 1.3 %reshape.30.bias_out_ref = f32[1,616]{1,0:T(1,128)} reshape(f32[616]{0:T(1024)} %param.30) | data formatting | bytes 4928 | tf_op jit(solution)/shard_map/reshape | solution.py:466
  2.6 0.7 convert_bitcast_fusion
  3.3 0.0 copy-start
  3.3 1.4 %pad_maximum_fusion.table_ref = f32[16,512]{1,0:T(8,128)} fusion(f32[8,512]{1,0:T(8,128)S(1)} %broadcast_in_dim.2, f32[4,512]{1,0:T(4,128)} %bitcast.12, f32[4,512]{1,0:T(4,128)S(1)} %convert_bitcast_fusion), kind=kLoop, calls=%fused_computation | loop fusion | flops 16384 | bytes 65536 | tf_op jit(solution)/shard_map/concatenate | solution.py:403
  4.7 2.8 %copy.17.observations_hbm = f32[512,616]{1,0:T(8,128)} copy(f32[512,616]{0,1:T(8,128)} %param.25) | data formatting | bytes 2523136 | tf_op args[9]
  7.5 0.0 copy-done
  7.5 1.4 %copy.18.layer_out_hbm = bf16[1024,616]{1,0:T(8,128)(2,1)} copy(bf16[1024,616]{0,1:T(8,128)(2,1)S(1)} %copy-done) | data formatting | bytes 2523136 | tf_op args[13]
  9.0 63.9 %step.1 = f32[4,512,128]{2,1,0:T(8,128)} custom-call(f32[16,512]{1,0:T(8,128)} %pad_maximum_fusion.table_ref, s32[1]{0:T(128)S(6)} %copy.20.live_ref, f32[1,128]{1,0:T(1,128)} %bitcast.14, f32[1,128]{1,0:T(1,128)} %bitcast.15, f32[1,1024]{1,0:T(1,128)} %bitcast.13, f32[1,616]{1,0:T(1,128)} %reshape.30.bias_out_ref, f32[4,512,128]{2,1,0:T(8,128)} %state_hbm.1, ...), custom_call_target="tpu_custom_call" | custom-call | tf_op jit(solution)/shard_map/step/pallas_call | solution.py:414
  72.8 2.3 %copy.21 = f32[4,512,128]{2,1,0:T(8,128)} copy(f32[4,512,128]{2,1,0:T(8,128)} %step.1) | data formatting | bytes 2097152
  (1 shorter events, 0.0 us)
Async XLA Ops:
  3.3 4.2 %copy-start = (bf16[1024,616]{0,1:T(8,128)(2,1)S(1)}, bf16[1024,616]{0,1:T(8,128)(2,1)}, u32[]{:S(2)}) copy-start(bf16[1024,616]{0,1:T(8,128)(2,1)} %param.29) | copy-start | bytes 3784708
where the time goes:
time: 75.5 us; the launch traced here: 75.1 us
  Pallas kernels  63.9 us (85%)
  local copies, waits for them, and re-layouts  7.76 us (10%)
  other arithmetic  2.8 us (4%)
    pallas_call x1, Pallas kernels, per_device(): pl.pallas_call(functools.partial(kernel, n), out_shape=jax.ShapeDtypeStru...  63.9 us
    unnamed x5, local copies, waits for them, and re-layouts  6.48 us

commit v1 on v0

v1 whole, which is shorter than its diff:
```python
import functools

import jax
import jax.numpy as jnp
from jax import lax
from jax.experimental import pallas as pl
from jax.experimental.pallas import tpu as pltpu
from jax.sharding import PartitionSpec as P

F32 = jnp.float32
BF16 = jnp.bfloat16
MESH = pl.DeviceIdType.MESH
LANES = 128


def dot(a, b):
    return jnp.dot(a, b, preferred_element_type=F32)


def dot_nt(a, b):
    return lax.dot_general(a, b, (((1,), (1,)), ((), ())), preferred_element_type=F32)


def kernel(
    n,
    live_ref,
    state_hbm,
    background_hbm,
    back_precision_hbm,
    conv_first_hbm,
    bias_first_hbm,
    conv_second_hbm,
    tile_hbm,
    cells_hbm,
    weights_hbm,
    observations_hbm,
    layer_in_hbm,
    bias_in_hbm,
    layer_out_hbm,
    bias_out_hbm,
    precision_hbm,
    out_ref,
    state_ref,
    background_ref,
    back_precision_ref,
    conv_first_ref,
    bias_first_ref,
    conv_second_ref,
    tile_ref,
    cells_ref,
    weights_ref,
    observations_ref,
    layer_in_ref,
    bias_in_ref,
    layer_out_ref,
    bias_out_ref,
    precision_ref,
    pair_first_ref,
    pair_second_ref,
    adj_first_ref,
    adj_second_ref,
    offset_ref,
    product_ref,
    field_ref,
    halo_ref,
    taps_ref,
    hidden_ref,
    hidden_taps_ref,
    partial_ref,
    edge_ref,
    observed_t_ref,
    values_ref,
    place_ref,
    place_t_ref,
    share_t_ref,
    grad_ref,
    req_src,
    req_dst,
    ret_src,
    ret_dst,
    out_src,
    out_dst,
    load_sem,
    halo_send,
    halo_recv,
    req_send,
    req_recv,
    ret_send,
    ret_recv,
    out_send,
    out_recv,
):
    me = lax.axis_index("dev")
    rows, cols, ch = state_ref.shape
    slots, listed = place_t_ref.shape
    cap = slots // n
    per = LANES // cap
    groups = slots // LANES
    half = n // 2
    span_half = slots // 2
    wide = 3 * ch
    margin = cells_ref.shape[0]
    my_half = lax.div(me, half)

    loads = [
        pltpu.make_async_copy(src, dst, load_sem.at[i])
        for i, (src, dst) in enumerate(
            (
                (tile_hbm, tile_ref),
                (cells_hbm, cells_ref),
                (weights_hbm, weights_ref),
                (state_hbm, state_ref),
                (conv_first_hbm, conv_first_ref),
                (bias_first_hbm, bias_first_ref),
                (precision_hbm, precision_ref),
                (layer_out_hbm, layer_out_ref),
                (conv_second_hbm, conv_second_ref),
                (observations_hbm, observations_ref),
                (bias_out_hbm, bias_out_ref),
                (background_hbm, background_ref),
                (back_precision_hbm, back_precision_ref),
                (layer_in_hbm, layer_in_ref),
                (bias_in_hbm, bias_in_ref),
            )
        )
    ]
    for load in loads:
        load.start()

    barrier = pltpu.get_barrier_semaphore()

    def greet(k, carry):
        pl.semaphore_signal(
            barrier, inc=1, device_id=(lax.rem(me + k, n),), device_id_type=MESH
        )
        return carry

    lax.fori_loop(1, n, greet, 0)

    def post(src, dst, send, recv, target):
        k = lax.rem(target + n - me, n)
        pltpu.make_async_remote_copy(
            src_ref=src.at[target],
            dst_ref=dst.at[me],
            send_sem=send.at[k],
            recv_sem=recv.at[k],
            device_id=(target,),
            device_id_type=MESH,
        ).start()

    def exchange_far(*refs):
        def start(j, carry):
            post(*refs, (1 - my_half) * half + lax.rem(me + j, half))
            return carry

        lax.fori_loop(0, half, start, 0)

    def exchange_near(*refs):
        def start(j, carry):
            post(*refs, my_half * half + lax.rem(me + j, half))
            return carry

        lax.fori_loop(1, half, start, 0)

    def settle(src, dst, send, recv):
        def wait(k, carry):
            copy = pltpu.make_async_remote_copy(
                src_ref=src.at[lax.rem(me + k, n)],
                dst_ref=dst.at[lax.rem(me + n - k, n)],
                send_sem=send.at[k],
                recv_sem=recv.at[k],
                device_id=(lax.rem(me + k, n),),
                device_id_type=MESH,
            )
            copy.wait_recv()
            copy.wait_send()
            return carry

        lax.fori_loop(1, n, wait, 0)

    def rim(phase, side, depth):
        row = (rows - 1 - depth) if side == 0 else depth
        return pltpu.make_async_remote_copy(
            src_ref=field_ref.at[phase, row],
            dst_ref=halo_ref.at[phase, side, depth],
            send_sem=halo_send.at[phase, side, depth],
            recv_sem=halo_recv.at[phase, side, depth],
            device_id=(lax.rem(me + 1, n) if side == 0 else lax.rem(me + n - 1, n),),
            device_id_type=MESH,
        )

    sends = (me < n - 1, me > 0)
    gets = (me > 0, me < n - 1)

    def rim_start(phase, depth):
        for side in range(2):

            @pl.when(sends[side])
            def _():
                rim(phase, side, depth).start()

    def rim_sent(phase, depth):
        for side in range(2):

            @pl.when(sends[side])
            def _():
                rim(phase, side, depth).wait_send()

    def put_taps(taps, slot, value):
        base = slot * wide
        taps[:, pl.ds(base, ch)] = pltpu.roll(value, 1, 0).astype(BF16)
        taps[:, pl.ds(base + ch, ch)] = value.astype(BF16)
        taps[:, pl.ds(base + 2 * ch, ch)] = pltpu.roll(value, cols - 1, 0).astype(BF16)

    def rim_take(phase, depth):
        for side in range(2):
            slot = (1 - depth) if side == 0 else rows + 2 + depth

            @pl.when(gets[side])
            def _():
                rim(phase, side, depth).wait_recv()
                put_taps(taps_ref, slot, halo_ref[phase, side, depth].astype(F32))

            @pl.when(jnp.logical_not(gets[side]))
            def _():
                taps_ref[:, pl.ds(slot * wide, wide)] = jnp.zeros((cols, wide), BF16)

    def make_pair(pair_ref, tap):
        zero = jnp.zeros((wide, ch), BF16)
        for a in range(4):
            for o in range(2):
                if 0 <= a - o < 3:
                    for b in range(3):
                        pair_ref[pl.ds(a * wide + b * ch, ch), pl.ds(o * ch, ch)] = tap(a - o, b)
                else:
                    pair_ref[pl.ds(a * wide, wide), pl.ds(o * ch, ch)] = zero

    def plain_of(ref):
        return lambda a, b: ref[a, pl.ds(b * ch, ch)]

    def adjoint_of(ref):
        return lambda a, b: ref[2 - a, pl.ds((2 - b) * ch, ch)].astype(F32).T.astype(BF16)

    def pair_all(taps, slot, pair):
        return dot(taps[:, pl.ds(slot * wide, 4 * wide)], pair[...])

    def pair_lower(taps, slot, pair):
        return dot(taps[:, pl.ds((slot + 1) * wide, 3 * wide)], pair[pl.ds(wide, 3 * wide)])

    def pair_upper(taps, slot, pair):
        return dot(taps[:, pl.ds(slot * wide, 3 * wide)], pair[pl.ds(0, 3 * wide)])

    def first_tap(taps, slot, pair):
        return dot(taps[:, pl.ds(slot * wide, wide)], pair[pl.ds(0, wide), pl.ds(0, ch)])

    def last_tap(taps, slot, pair):
        return dot(taps[:, pl.ds((slot + 2) * wide, wide)], pair[pl.ds(3 * wide, wide), pl.ds(ch, ch)])

    def outer_inside(pair, put):
        for slot in range(2, rows, 2):
            both = pair_all(taps_ref, slot, pair)
            put(slot, both[:, :ch])
            put(slot + 1, both[:, ch:])

    def outer_near(pair, put):
        both = pair_lower(taps_ref, 0, pair)
        partial_ref[0] = both[:, :ch]
        put(1, both[:, ch:])
        both = pair_upper(taps_ref, rows, pair)
        put(rows, both[:, :ch])
        partial_ref[1] = both[:, ch:]

    def outer_far(pair, put):
        put(0, (partial_ref[0] + first_tap(taps_ref, 0, pair)) * gets[0].astype(F32))
        put(rows + 1, (partial_ref[1] + last_tap(taps_ref, rows + 1, pair)) * gets[1].astype(F32))

    def inner_near(pair, put, put_edge):
        both = pair_lower(hidden_taps_ref, 0, pair)
        put_edge(0, both[:, :ch])
        put(1, both[:, ch:])
        for slot in range(2, rows - 2, 2):
            both = pair_all(hidden_taps_ref, slot, pair)
            put(slot, both[:, :ch])
            put(slot + 1, both[:, ch:])
        both = pair_upper(hidden_taps_ref, rows - 2, pair)
        put(rows - 2, both[:, :ch])
        put_edge(1, both[:, ch:])

    for load in loads[0:3]:
        load.wait()
    tile_row = tile_ref[...].astype(F32)
    tile_col = jnp.broadcast_to(tile_row, (LANES, listed)).T[:, 0:1]
    same = tile_col == tile_row
    from_col = lax.broadcasted_iota(jnp.int32, (listed, listed), 0)
    from_row = lax.broadcasted_iota(jnp.int32, (listed, listed), 1)
    rank_row = jnp.sum(jnp.where(same & (from_col < from_row), 1.0, 0.0), axis=0, keepdims=True)
    slot_row = (tile_row * cap + rank_row).astype(jnp.int32)
    for g in range(groups):
        rowid = lax.broadcasted_iota(jnp.int32, (LANES, listed), 0) + g * LANES
        place_t_ref[pl.ds(g * LANES, LANES)] = jnp.where(rowid == slot_row, 1.0, 0.0).astype(BF16)

    values_ref[0:margin] = cells_ref[...].astype(F32)
    values_ref[margin : 2 * margin] = weights_ref[...]
    values = values_ref[...]
    part_1 = values.astype(BF16).astype(F32)
    part_2 = (values - part_1).astype(BF16).astype(F32)
    part_3 = values - part_1 - part_2
    parts = jnp.concatenate([part_1, part_2, part_3, jnp.zeros_like(values)], axis=0).astype(BF16)
    own_lanes = lax.broadcasted_iota(jnp.int32, (8, LANES), 1) // cap == lax.rem(me, per)
    for g in range(groups):
        spread = dot_nt(parts, place_t_ref[pl.ds(g * LANES, LANES)])
        spread = spread[0:8] + spread[8:16] + spread[16:24]
        for i in range(per):
            turned = pltpu.roll(spread, lax.rem(lax.rem(me, per) + per - i, per) * cap, 1)
            req_src[g * per + i] = jnp.where(own_lanes, turned, 0.0)
    req_dst[me] = req_src[me]

    loads[3].wait()
    for r in range(rows):
        value = state_ref[r].astype(BF16)
        field_ref[0, r] = value
        put_taps(taps_ref, r + 2, value.astype(F32))

    def put_hidden(slot, value):
        inside = {0: gets[0], rows + 1: gets[1]}.get(slot)
        value = jnp.tanh(value + bias_first_ref[...]).astype(BF16).astype(F32)
        if inside is not None:
            value = value * inside.astype(F32)
        hidden_ref[slot] = value
        put_taps(hidden_taps_ref, slot, value)

    loads[4].wait()
    loads[5].wait()
    make_pair(pair_first_ref, plain_of(conv_first_ref))
    outer_inside(pair_first_ref, put_hidden)

    pl.semaphore_wait(barrier, n - 1)
    rim_start(0, 0)
    req = (req_src, req_dst, req_send, req_recv)
    exchange_far(*req)
    exchange_near(*req)
    rim_start(0, 1)

    loads[6].wait()
    loads[7].wait()
    chan = precision_ref.shape[0]
    step = 2 * LANES
    for s in range(0, chan, step):
        size = min(step, chan - s)
        wanted_rows = precision_ref[pl.ds(s, size)]
        high = wanted_rows.astype(BF16)
        low = (wanted_rows - high.astype(F32)).astype(BF16)
        product_ref[pl.ds(s, size)] = (
            dot(high, layer_out_ref[...]) + dot(low, layer_out_ref[...])
        ).astype(BF16)
    loads[8].wait()
    make_pair(pair_second_ref, plain_of(conv_second_ref))

    settle(*req)
    wanted = []
    for g in range(groups):
        total = req_dst[g * per]
        for i in range(1, per):
            total = total + req_dst[g * per + i]
        wanted.append(total)

    def build_shares(c, carry):
        base = pl.multiple_of(c * LANES, LANES)
        cell = lax.broadcasted_iota(jnp.int32, (LANES, LANES), 0).astype(F32)
        for g in range(groups):
            local = wanted[g] - base.astype(F32)
            total = jnp.zeros((LANES, LANES), F32)
            for k in range(margin):
                total = total + jnp.where(
                    cell == local[k : k + 1], wanted[g][margin + k : margin + k + 1], 0.0
                )
            share_t_ref[pl.ds(base, LANES), pl.ds(g * LANES, LANES)] = total.astype(BF16)
        return carry

    lax.fori_loop(0, rows * cols // LANES, build_shares, 0)

    rim_take(0, 0)
    outer_near(pair_first_ref, put_hidden)

    def put_observed(r, value):
        value = state_ref[r] + value
        observed_t_ref[:, pl.ds(r * cols, cols)] = value.T.astype(BF16)

    def hold_edge(side, value):
        edge_ref[side] = value

    inner_near(pair_second_ref, put_observed, hold_edge)
    rim_take(0, 1)

    def outer_far_forward():
        put_hidden(0, partial_ref[0] + first_tap(taps_ref, 0, pair_first_ref))
        put_hidden(rows + 1, partial_ref[1] + last_tap(taps_ref, rows + 1, pair_first_ref))

    outer_far_forward()
    put_observed(0, edge_ref[0] + first_tap(hidden_taps_ref, 0, pair_second_ref))
    put_observed(rows - 1, edge_ref[1] + last_tap(hidden_taps_ref, rows - 1, pair_second_ref))

    ret = (ret_src, ret_dst, ret_send, ret_recv)

    def blend(which):
        base = pl.multiple_of(which * span_half, span_half)
        blended = dot(observed_t_ref[...], share_t_ref[:, pl.ds(base, span_half)]).T
        ret_src[pl.ds(which * half, half)] = blended.reshape(half, cap, ch).astype(BF16)

    blend(1 - my_half)
    exchange_far(*ret)
    blend(my_half)
    exchange_near(*ret)
    ret_dst[me] = ret_src[me]

    rank_col = jnp.sum(jnp.where(same & (from_row < from_col), 1.0, 0.0), axis=1, keepdims=True)
    slot_col = (tile_col * cap + rank_col).astype(jnp.int32)
    for g in range(groups):
        colid = lax.broadcasted_iota(jnp.int32, (listed, LANES), 1) + g * LANES
        place_ref[:, pl.ds(g * LANES, LANES)] = jnp.where(colid == slot_col, 1.0, 0.0).astype(BF16)
    loads[9].wait()
    loads[10].wait()
    bias_out = bias_out_ref[...].reshape(1, -1)
    for s in range(0, listed, LANES):
        offset_ref[pl.ds(s, LANES)] = bias_out - observations_ref[:, pl.ds(s, LANES)].T
    make_pair(adj_second_ref, adjoint_of(conv_second_ref))
    make_pair(adj_first_ref, adjoint_of(conv_first_ref))
    loads[11].wait()
    loads[12].wait()
    for r in range(rows):
        out_ref[r] = back_precision_ref[...] * (state_ref[r] - background_ref[r])
    loads[13].wait()
    loads[14].wait()

    settle(*ret)
    returned = ret_dst[...].astype(F32).reshape(slots, ch).astype(BF16)
    live = live_ref[0]
    block = listed // 2
    for s in range(0, listed, block):
        span = pl.ds(s, block)
        interpolated = dot(place_ref[span], returned).astype(BF16)
        activated = jnp.tanh(dot(interpolated, layer_in_ref[...]) + bias_in_ref[...]).astype(BF16)
        innovation = dot_nt(activated, layer_out_ref[...]) + offset_ref[span]
        alive = lax.broadcasted_iota(jnp.int32, (block, 1), 0) + s < live
        innovation = jnp.where(alive, innovation, 0.0)
        back_act = dot(innovation.astype(BF16), product_ref[...])
        act_wide = activated.astype(F32)
        pre_grad = (back_act * (1.0 - act_wide * act_wide)).astype(BF16)
        grad_ref[span] = dot_nt(pre_grad, layer_in_ref[...]).astype(BF16)

    out = (out_src, out_dst, out_send, out_recv)

    def dispatch(which):
        base = pl.multiple_of(which * span_half, span_half)
        outgoing = dot(place_t_ref[pl.ds(base, span_half)], grad_ref[...])
        out_src[pl.ds(which * half, half)] = outgoing.reshape(half, cap, ch).astype(BF16)

    dispatch(1 - my_half)
    exchange_far(*out)
    dispatch(my_half)
    exchange_near(*out)
    out_dst[me] = out_src[me]
    settle(*out)
    arrived = out_dst[...].astype(F32).reshape(slots, ch).astype(BF16)

    def gather_grad(r):
        value = dot(share_t_ref[pl.ds(r * cols, cols)], arrived)
        out_ref[r] = out_ref[r] + value
        value = value.astype(BF16)
        field_ref[1, r] = value
        put_taps(taps_ref, r + 2, value.astype(F32))

    gather_grad(0)
    gather_grad(rows - 1)
    rim_start(1, 0)
    for r in range(1, rows - 1):
        gather_grad(r)
    rim_start(1, 1)

    def put_act(slot, value):
        hidden = hidden_ref[slot]
        value = value * (1.0 - hidden * hidden)
        put_taps(hidden_taps_ref, slot, value.astype(BF16).astype(F32))

    def add_out(r, value):
        out_ref[r] = out_ref[r] + value

    def add_edge(side, value):
        add_out(0 if side == 0 else rows - 1, value)

    outer_inside(adj_second_ref, put_act)
    rim_take(1, 0)
    outer_near(adj_second_ref, put_act)
    inner_near(adj_first_ref, add_out, add_edge)
    rim_take(1, 1)
    outer_far(adj_second_ref, put_act)
    add_out(0, first_tap(hidden_taps_ref, 0, adj_first_ref))
    add_out(rows - 1, last_tap(hidden_taps_ref, rows - 1, adj_first_ref))
    for phase in range(2):
        for depth in range(2):
            rim_sent(phase, depth)


def per_device(
    state,
    background,
    back_precision,
    conv_first,
    bias_first,
    conv_second,
    sounding_tile,
    sounding_cells,
    cell_weights,
    observations,
    live_counts,
    layer_in,
    bias_in,
    layer_out,
    bias_out,
    error_precision,
):
    rows, cols, ch = state.shape
    n = lax.axis_size("dev")
    listed = sounding_tile.shape[0]
    margin = sounding_cells.shape[1]
    slots = 2 * listed
    cap = slots // n
    hid, chan = layer_out.shape
    vmem = pl.BlockSpec(memory_space=pltpu.VMEM)
    hbm = pl.BlockSpec(memory_space=pltpu.HBM)
    dma = pltpu.SemaphoreType.DMA
    operands = tuple(pltpu.with_memory_space_constraint(x, pltpu.HBM) for x in (
        state,
        background,
        back_precision.reshape(1, -1),
        conv_first.reshape(3, 3 * ch, ch),
        bias_first.reshape(1, -1),
        conv_second.reshape(3, 3 * ch, ch),
        sounding_tile.T,
        sounding_cells.T,
        cell_weights.T,
        observations.T,
        layer_in,
        bias_in.reshape(1, -1),
        layer_out.T,
        bias_out,
        error_precision,
    ))
    return pl.pallas_call(
        functools.partial(kernel, n),
        out_shape=jax.ShapeDtypeStruct(state.shape, F32),
        in_specs=[pl.BlockSpec(memory_space=pltpu.SMEM)] + [hbm] * len(operands),
        out_specs=vmem,
        scratch_shapes=[pltpu.VMEM(x.shape, x.dtype) for x in operands]
        + [pltpu.VMEM((12 * ch, 2 * ch), BF16)] * 4
        + [
            pltpu.VMEM((listed, chan), F32),
            pltpu.VMEM((chan, hid), BF16),
            pltpu.VMEM((2, rows, cols, ch), BF16),
            pltpu.VMEM((2, 2, 2, cols, ch), BF16),
            pltpu.VMEM((cols, (rows + 4) * 3 * ch), BF16),
            pltpu.VMEM((rows + 2, cols, ch), F32),
            pltpu.VMEM((cols, (rows + 2) * 3 * ch), BF16),
            pltpu.VMEM((2, cols, ch), F32),
            pltpu.VMEM((2, cols, ch), F32),
            pltpu.VMEM((ch, rows * cols), BF16),
            pltpu.VMEM((2 * margin, listed), F32),
            pltpu.VMEM((listed, slots), BF16),
            pltpu.VMEM((slots, listed), BF16),
            pltpu.VMEM((rows * cols, slots), BF16),
            pltpu.VMEM((listed, ch), BF16),
            pltpu.VMEM((n, 8, LANES), F32),
            pltpu.VMEM((n, 8, LANES), F32),
            pltpu.VMEM((n, cap, ch), BF16),
            pltpu.VMEM((n, cap, ch), BF16),
            pltpu.VMEM((n, cap, ch), BF16),
            pltpu.VMEM((n, cap, ch), BF16),
            dma((len(operands),)),
            dma((2, 2, 2)),
            dma((2, 2, 2)),
            dma((n,)),
            dma((n,)),
            dma((n,)),
            dma((n,)),
            dma((n,)),
            dma((n,)),
        ],
        compiler_params=pltpu.CompilerParams(
            collective_id=0, has_side_effects=True, vmem_limit_bytes=48 * 1024 * 1024
        ),
        name="step",
    )(live_counts, *operands)


def solution(mesh):
    split = P("dev")
    return jax.shard_map(
        per_device,
        mesh=mesh,
        in_specs=(
            split, split, P(), P(), P(), P(), split, split, split, split, split, P(), P(), P(), P(), P(),
        ),
        out_specs=split,
        check_vma=False,
    )
```

time: 75.5 us -> 54 us (0.72)
  the two profiles are of different devices: /device:TPU:0 before, /device:TPU:1 now
where the time goes in v1:
time: 54 us; the launch traced here: 53.8 us
  Pallas kernels  52.2 us (97%)
  local copies, waits for them, and re-layouts  0.97 us (2%)
  between operations  0.66 us (1%)
    pallas_call x1, Pallas kernels, per_device(): pl.pallas_call(functools.partial(kernel, n), out_shape=jax.ShapeDtypeStru...  52.2 us

profile of v1, /device:TPU:1, one launch (start us, length us, event | category | flops | bytes accessed | tf_op | source)
XLA Modules:
  0.0 53.8 jit_solution(16097867118851090293)
XLA Ops:
  0.7 52.2 %step.1 = f32[4,512,128]{2,1,0:T(8,128)S(1)} custom-call(s32[1]{0:T(128)S(6)} %copy.18.live_ref, f32[4,512,128]{2,1,0:T(8,128)} %state_hbm.1, f32[4,512,128]{2,1,0:T(8,128)} %background_hbm.1, f32[1,128]{1,0:T(1,128)} %bitcast.18, bf16[3,384,128]{2,1,0:T(8,128)(2,1)} %bitcast.12, f32[1,128]{1,0:T(1,128)} %bitcast.19, bf16[3,384,128]{2,1,0:T(8,128)(2,1)} %bitcast.13, ...), custom_call_target="tpu_custom_call" | custom-call | tf_op jit(solution)/shard_map/step/pallas_call | solution.py:549
  52.8 1.0 %copy.19 = f32[4,512,128]{2,1,0:T(8,128)} copy(f32[4,512,128]{2,1,0:T(8,128)S(1)} %step.1) | data formatting | bytes 2097152

commit v2 on v1

v2 whole, which is shorter than its diff:
```python
import functools

import jax
import jax.numpy as jnp
from jax import lax
from jax.experimental import pallas as pl
from jax.experimental.pallas import tpu as pltpu
from jax.sharding import PartitionSpec as P

F32 = jnp.float32
BF16 = jnp.bfloat16
MESH = pl.DeviceIdType.MESH
LANES = 128


def dot(a, b):
    return jnp.dot(a, b, preferred_element_type=F32)


def dot_nt(a, b):
    return lax.dot_general(a, b, (((1,), (1,)), ((), ())), preferred_element_type=F32)


def kernel(
    n,
    live_ref,
    state_hbm,
    background_hbm,
    back_precision_hbm,
    conv_first_hbm,
    bias_first_hbm,
    conv_second_hbm,
    tile_hbm,
    cells_hbm,
    weights_hbm,
    observations_hbm,
    layer_in_hbm,
    bias_in_hbm,
    layer_out_hbm,
    bias_out_hbm,
    precision_hbm,
    out_ref,
    state_ref,
    background_ref,
    back_precision_ref,
    conv_first_ref,
    bias_first_ref,
    conv_second_ref,
    tile_ref,
    cells_ref,
    weights_ref,
    observations_ref,
    layer_in_ref,
    bias_in_ref,
    layer_out_ref,
    bias_out_ref,
    precision_ref,
    pair_first_ref,
    pair_second_ref,
    adj_first_ref,
    adj_second_ref,
    offset_ref,
    product_ref,
    field_ref,
    halo_ref,
    taps_ref,
    hidden_ref,
    hidden_taps_ref,
    partial_ref,
    edge_ref,
    local_ref,
    share_ref,
    observed_t_ref,
    values_ref,
    place_ref,
    place_t_ref,
    share_t_ref,
    grad_ref,
    req_src,
    req_dst,
    ret_src,
    ret_dst,
    out_src,
    out_dst,
    load_sem,
    halo_send,
    halo_recv,
    req_send,
    req_recv,
    ret_send,
    ret_recv,
    out_send,
    out_recv,
):
    me = lax.axis_index("dev")
    rows, cols, ch = state_ref.shape
    slots, listed = place_t_ref.shape
    cap = slots // n
    per = LANES // cap
    groups = slots // LANES
    half = n // 2
    wide = 3 * ch
    margin = cells_ref.shape[0]
    my_half = lax.div(me, half)
    quarter = n // 4
    my_quarter = lax.div(me, quarter)
    close = 1 - lax.rem(me, 2)

    loads = [
        pltpu.make_async_copy(src, dst, load_sem.at[i])
        for i, (src, dst) in enumerate(
            (
                (tile_hbm, tile_ref),
                (cells_hbm, cells_ref),
                (weights_hbm, weights_ref),
                (state_hbm, state_ref),
                (conv_first_hbm, conv_first_ref),
                (bias_first_hbm, bias_first_ref),
                (precision_hbm, precision_ref),
                (layer_out_hbm, layer_out_ref),
                (conv_second_hbm, conv_second_ref),
                (observations_hbm, observations_ref),
                (bias_out_hbm, bias_out_ref),
                (background_hbm, background_ref),
                (back_precision_hbm, back_precision_ref),
                (layer_in_hbm, layer_in_ref),
                (bias_in_hbm, bias_in_ref),
            )
        )
    ]
    barrier = pltpu.get_barrier_semaphore()

    def far_half(serve):
        def one(j, carry):
            serve((1 - my_half) * half + lax.rem(me + j, half))
            return carry

        lax.fori_loop(0, half, one, 0)

    def near_half(serve):
        def one(j, carry):
            serve(my_half * half + lax.rem(me + j, half))
            return carry

        lax.fori_loop(1, half, one, 0)

    def greet(target):
        pl.semaphore_signal(barrier, inc=1, device_id=(target,), device_id_type=MESH)

    for load in loads[:4]:
        load.start()
    far_half(greet)
    near_half(greet)
    for load in loads[4:]:
        load.start()

    def by_quarters(fill, serve):
        sub = lax.rem(my_quarter, 2)
        for step in range(4):
            which = (my_half if step > 1 else 1 - my_half) * 2 + lax.rem(sub + (step + step // 2) % 2, 2)
            fill(which)

            def one(j, carry):
                serve(which * quarter + lax.rem(me + j, quarter))
                return carry

            lax.fori_loop(1 if step == 3 else 0, quarter, one, 0)

    def post(src, dst, send, recv):
        def one(target):
            pltpu.make_async_remote_copy(
                src_ref=src.at[target],
                dst_ref=dst.at[me],
                send_sem=send,
                recv_sem=recv,
                device_id=(target,),
                device_id_type=MESH,
            ).start()

        return one

    def settle(dst, sem):
        blocks = dst.at[pl.ds(0, n - 1)]
        pltpu.make_async_copy(blocks, blocks, sem).wait()

    def rim(phase, side, depth):
        row = (1 - side) * (rows - 1 - depth) + side * depth
        return pltpu.make_async_remote_copy(
            src_ref=field_ref.at[phase, row],
            dst_ref=halo_ref.at[phase, side, depth],
            send_sem=halo_send.at[phase, side, depth],
            recv_sem=halo_recv.at[phase, side, depth],
            device_id=(lax.rem(me + 1 + side * (n - 2), n),),
            device_id_type=MESH,
        )

    sends = (me < n - 1, me > 0)

    def rim_start(phase, depth):
        for side in range(2):

            @pl.when(sends[side])
            def _():
                rim(phase, side, depth).start()

    def rim_sent(phase, depth):
        for side in range(2):

            @pl.when(sends[side])
            def _():
                rim(phase, side, depth).wait_send()

    def at(start, size):
        return pl.ds(start if isinstance(start, int) else pl.multiple_of(start, LANES), size)

    def put_taps(taps, slot, value):
        taps[:, at(slot * wide, ch)] = pltpu.roll(value, 1, 0).astype(BF16)
        taps[:, at(slot * wide + ch, ch)] = value.astype(BF16)
        taps[:, at(slot * wide + 2 * ch, ch)] = pltpu.roll(value, cols - 1, 0).astype(BF16)

    def rim_take(phase, side, depth):
        slot = 1 - depth + side * (rows + 1 + 2 * depth)

        met = me > 0 if side == 0 else me < n - 1

        @pl.when(met)
        def _():
            rim(phase, side, depth).wait_recv()
            put_taps(taps_ref, slot, halo_ref[phase, side, depth].astype(F32))

        @pl.when(jnp.logical_not(met))
        def _():
            taps_ref[:, pl.ds(slot * wide, wide)] = jnp.zeros((cols, wide), BF16)

    def make_pair(pair_ref, tap):
        zero = jnp.zeros((wide, ch), BF16)
        for a in range(4):
            for o in range(2):
                if 0 <= a - o < 3:
                    for b in range(3):
                        pair_ref[pl.ds(a * wide + b * ch, ch), pl.ds(o * ch, ch)] = tap(a - o, b)
                else:
                    pair_ref[pl.ds(a * wide, wide), pl.ds(o * ch, ch)] = zero

    def plain_of(ref):
        return lambda a, b: ref[a, pl.ds(b * ch, ch)]

    def adjoint_of(ref):
        return lambda a, b: ref[2 - a, pl.ds((2 - b) * ch, ch)].astype(F32).T.astype(BF16)

    def conv_inside(outer, put_outer, inner, put_inner):
        for slot in range(2, rows, 2):
            both = dot(taps_ref[:, pl.ds(slot * wide, 4 * wide)], outer[...])
            put_outer(slot, both[:, :ch])
            put_outer(slot + 1, both[:, ch:])
        for slot in range(2, rows - 2, 2):
            both = dot(hidden_taps_ref[:, pl.ds(slot * wide, 4 * wide)], inner[...])
            put_inner(slot, both[:, :ch])
            put_inner(slot + 1, both[:, ch:])

    def conv_one(side, phase, outer, put_outer, inner, put_inner):
        most = pl.ds((1 - side) * wide, 3 * wide)
        left = pl.ds(side * ch, ch)

        def halves(both):
            return (both[:, ch:], both[:, :ch])[:: 1 - 2 * side]

        rim_take(phase, side, 0)
        done, value = halves(dot(taps_ref[:, pl.ds((1 + side * (rows - 1)) * wide, 3 * wide)], outer[most]))
        partial_ref[...] = value
        put_outer(1 + side * (rows - 1), done)
        done, value = halves(dot(hidden_taps_ref[:, pl.ds((1 + side * (rows - 3)) * wide, 3 * wide)], inner[most]))
        edge_ref[...] = value
        put_inner(1 + side * (rows - 3), done)
        rim_take(phase, side, 1)
        last = pl.ds(side * 3 * wide, wide)
        value = partial_ref[...] + dot(taps_ref[:, pl.ds(side * (rows + 3) * wide, wide)], outer[last, left])
        put_outer(side * (rows + 1), value, (me > 0 if side == 0 else me < n - 1).astype(F32))
        value = edge_ref[...] + dot(hidden_taps_ref[:, pl.ds(side * (rows + 1) * wide, wide)], inner[last, left])
        put_inner(side * (rows - 1), value)

    def conv_side(which, *refs):
        for side in range(2):

            @pl.when(which == side)
            def _():
                conv_one(side, *refs)

    for load in loads[0:3]:
        load.wait()
    tile_row = tile_ref[...].astype(F32)
    tile_col = jnp.broadcast_to(tile_row, (LANES, listed)).T[:, 0:1]
    same = tile_col == tile_row
    from_col = lax.broadcasted_iota(jnp.int32, (listed, listed), 0)
    from_row = lax.broadcasted_iota(jnp.int32, (listed, listed), 1)
    rank_row = jnp.sum(jnp.where(same & (from_col < from_row), 1.0, 0.0), axis=0, keepdims=True)
    slot_row = (tile_row * cap + rank_row).astype(jnp.int32)
    for g in range(groups):
        rowid = lax.broadcasted_iota(jnp.int32, (LANES, listed), 0) + g * LANES
        place_t_ref[pl.ds(g * LANES, LANES)] = jnp.where(rowid == slot_row, 1.0, 0.0).astype(BF16)

    block_of = lax.broadcasted_iota(jnp.int32, (8, LANES), 1) // cap
    row_of = lax.broadcasted_iota(jnp.int32, (8, LANES), 0)
    values_ref[0:margin] = cells_ref[...].astype(F32)
    values_ref[margin : 2 * margin] = weights_ref[...]
    values = values_ref[...]
    part_1 = values.astype(BF16).astype(F32)
    part_2 = (values - part_1).astype(BF16).astype(F32)
    part_3 = values - part_1 - part_2
    parts = jnp.concatenate([part_1, part_2, part_3, jnp.zeros_like(values)], axis=0).astype(BF16)
    held = 2 * margin
    packed = min(held, per)
    on_k = [
        (block_of == k) & (row_of % packed == k) for k in range(packed)
    ]
    for g in range(groups):
        spread = dot_nt(parts, place_t_ref[pl.ds(g * LANES, LANES)])
        spread = spread[0:8] + spread[8:16] + spread[16:24]
        turned = [spread] + [pltpu.roll(spread, d * cap, 1) for d in range(1, per)]
        for i in range(per):
            total = jnp.zeros_like(spread)
            for k in range(packed):
                total = jnp.where(on_k[k], turned[(k + per - i) % per], total)
            reach = 1
            while reach < packed:
                total = total + pltpu.roll(total, held - reach, 0)
                reach = 2 * reach
            for h in range(held // packed):
                req_src[g * per + i, :, pl.ds(h * LANES, LANES)] = total[h * packed : h * packed + 1]
    req_dst[me] = req_src[me]

    loads[3].wait()
    for r in range(rows):
        value = state_ref[r].astype(BF16)
        field_ref[0, r] = value
        put_taps(taps_ref, r + 2, value.astype(F32))

    def put_hidden(slot, value, keep=None):
        value = jnp.tanh(value + bias_first_ref[...]).astype(BF16).astype(F32)
        if keep is not None:
            value = value * keep
        hidden_ref[slot] = value
        put_taps(hidden_taps_ref, slot, value)

    def put_observed(r, value):
        value = state_ref[r] + value
        observed_t_ref[:, at(r * cols, cols)] = value.T.astype(BF16)

    forward = (pair_first_ref, put_hidden, pair_second_ref, put_observed)

    pl.semaphore_wait(barrier, n - 1)
    far_half(post(req_src, req_dst, req_send, req_recv))
    near_half(post(req_src, req_dst, req_send, req_recv))
    rim_start(0, 0)
    rim_start(0, 1)

    loads[4].wait()
    loads[5].wait()
    make_pair(pair_first_ref, plain_of(conv_first_ref))
    loads[8].wait()
    make_pair(pair_second_ref, plain_of(conv_second_ref))

    conv_inside(*forward)
    conv_side(close, 0, *forward)
    settle(req_dst, req_recv)
    for g in range(groups):
        sent = []
        for i in range(per):
            total = jnp.zeros((held, LANES), F32)
            for h in range(held // packed):
                row = jnp.broadcast_to(req_dst[g * per + i, :, pl.ds(h * LANES, LANES)], (held, LANES))
                total = jnp.where(row_of // packed == h, row, total)
            sent.append(total)
        total = jnp.zeros((held, LANES), F32)
        for d in range(per):
            part = jnp.zeros((held, LANES), F32)
            for k in range(packed):
                part = jnp.where(on_k[k], sent[(k + d) % per], part)
            total = total + (pltpu.roll(part, d * cap, 1) if d else part)

        cell = total[0:margin]
        chunk = jnp.floor(cell * (1.0 / LANES))
        local_ref[g] = jnp.concatenate([cell - chunk * LANES, chunk], axis=0)
        share_ref[g] = jnp.concatenate([total[margin:], total[margin:]], axis=0)

    def build_shares(g, carry):
        packs = (LANES // 16, 16, LANES)
        cell = lax.broadcasted_iota(jnp.int32, packs, 0) * 16 + lax.broadcasted_iota(jnp.int32, packs, 1)
        cell = cell.astype(F32).astype(BF16)

        def spread_row(row):
            return jnp.broadcast_to(row, (16, LANES)).astype(BF16)[None]

        local = local_ref[g]
        share = share_ref[g][0:margin]
        hit = [
            jnp.where(cell == spread_row(local[k : k + 1]), 1.0, 0.0).astype(BF16)
            for k in range(margin)
        ]
        for c in range(rows * cols // LANES):
            here = jnp.where(local[margin:] == c, share, 0.0)
            total = hit[0] * spread_row(here[0:1])
            for k in range(1, margin):
                total = total + hit[k] * spread_row(here[k : k + 1])
            share_t_ref[pl.ds(c * LANES, LANES), at(g * LANES, LANES)] = total.reshape(LANES, LANES)
        return carry

    lax.fori_loop(0, groups, build_shares, 0)
    conv_side(1 - close, 0, *forward)

    ret = post(ret_src, ret_dst, ret_send, ret_recv)

    def blend(which):
        base = which * (slots // 2)
        blended = dot(observed_t_ref[...], share_t_ref[:, at(base, slots // 2)]).T
        ret_src[pl.ds(which * half, half)] = blended.reshape(half, cap, ch).astype(BF16)

    blend(1 - my_half)
    far_half(ret)
    blend(my_half)
    near_half(ret)
    ret_dst[me] = ret_src[me]

    rank_col = jnp.sum(jnp.where(same & (from_row < from_col), 1.0, 0.0), axis=1, keepdims=True)
    slot_col = (tile_col * cap + rank_col).astype(jnp.int32)
    for g in range(groups):
        colid = lax.broadcasted_iota(jnp.int32, (listed, LANES), 1) + g * LANES
        place_ref[:, pl.ds(g * LANES, LANES)] = jnp.where(colid == slot_col, 1.0, 0.0).astype(BF16)
    make_pair(adj_second_ref, adjoint_of(conv_second_ref))
    make_pair(adj_first_ref, adjoint_of(conv_first_ref))

    loads[9].wait()
    loads[10].wait()
    bias_out = bias_out_ref[...].reshape(1, -1)
    for s in range(0, listed, LANES):
        offset_ref[pl.ds(s, LANES)] = bias_out - observations_ref[:, pl.ds(s, LANES)].T
    loads[11].wait()
    loads[12].wait()
    for r in range(rows):
        out_ref[r] = back_precision_ref[...] * (state_ref[r] - background_ref[r])
    loads[13].wait()
    loads[14].wait()

    loads[6].wait()
    loads[7].wait()
    chan = precision_ref.shape[0]
    step = 2 * LANES
    for s in range(0, chan, step):
        size = min(step, chan - s)
        wanted_rows = precision_ref[pl.ds(s, size)]
        high = wanted_rows.astype(BF16)
        low = (wanted_rows - high.astype(F32)).astype(BF16)
        product_ref[pl.ds(s, size)] = (
            dot(high, layer_out_ref[...]) + dot(low, layer_out_ref[...])
        ).astype(BF16)

    def flat(ref):
        if cap % 16 == 0:
            return ref[...].reshape(slots, ch)
        return ref[...].astype(F32).reshape(slots, ch).astype(BF16)

    settle(ret_dst, ret_recv)
    returned = flat(ret_dst)
    live = live_ref[0]
    block = listed // 2
    for s in range(0, listed, block):
        span = pl.ds(s, block)
        interpolated = dot(place_ref[span], returned).astype(BF16)
        activated = jnp.tanh(dot(interpolated, layer_in_ref[...]) + bias_in_ref[...]).astype(BF16)
        innovation = dot_nt(activated, layer_out_ref[...]) + offset_ref[span]
        alive = lax.broadcasted_iota(jnp.int32, (block, 1), 0) + s < live
        innovation = jnp.where(alive, innovation, 0.0)
        back_act = dot(innovation.astype(BF16), product_ref[...])
        act_wide = activated.astype(F32)
        pre_grad = (back_act * (1.0 - act_wide * act_wide)).astype(BF16)
        grad_ref[span] = dot_nt(pre_grad, layer_in_ref[...]).astype(BF16)

    out = post(out_src, out_dst, out_send, out_recv)

    def dispatch(which):
        base = which * (slots // 4)
        outgoing = dot(place_t_ref[at(base, slots // 4)], grad_ref[...])
        out_src[pl.ds(which * quarter, quarter)] = outgoing.reshape(quarter, cap, ch).astype(BF16)

    by_quarters(dispatch, out)
    out_dst[me] = out_src[me]
    settle(out_dst, out_recv)
    arrived = flat(out_dst)

    def gather_grad(r):
        value = dot(share_t_ref[pl.ds(r * cols, cols)], arrived)
        out_ref[r] = out_ref[r] + value
        value = value.astype(BF16)
        field_ref[1, r] = value
        put_taps(taps_ref, r + 2, value.astype(F32))

    gather_grad(0)
    gather_grad(rows - 1)
    rim_start(1, 0)
    for r in range(1, rows - 1):
        gather_grad(r)
    rim_start(1, 1)

    def put_act(slot, value, keep=None):
        hidden = hidden_ref[slot]
        value = value * (1.0 - hidden * hidden)
        if keep is not None:
            value = value * keep
        put_taps(hidden_taps_ref, slot, value.astype(BF16).astype(F32))

    def add_out(r, value):
        out_ref[r] = out_ref[r] + value

    backward = (adj_second_ref, put_act, adj_first_ref, add_out)
    conv_inside(*backward)
    conv_side(close, 1, *backward)
    conv_side(1 - close, 1, *backward)
    for phase in range(2):
        for depth in range(2):
            rim_sent(phase, depth)
    settle(req_src, req_send)
    settle(ret_src, ret_send)
    settle(out_src, out_send)


def per_device(
    state,
    background,
    back_precision,
    conv_first,
    bias_first,
    conv_second,
    sounding_tile,
    sounding_cells,
    cell_weights,
    observations,
    live_counts,
    layer_in,
    bias_in,
    layer_out,
    bias_out,
    error_precision,
):
    rows, cols, ch = state.shape
    n = lax.axis_size("dev")
    listed = sounding_tile.shape[0]
    margin = sounding_cells.shape[1]
    slots = 2 * listed
    cap = slots // n
    hid, chan = layer_out.shape
    vmem = pl.BlockSpec(memory_space=pltpu.VMEM)
    hbm = pl.BlockSpec(memory_space=pltpu.HBM)
    dma = pltpu.SemaphoreType.DMA
    operands = tuple(pltpu.with_memory_space_constraint(x, pltpu.HBM) for x in (
        state,
        background,
        back_precision.reshape(1, -1),
        conv_first.reshape(3, 3 * ch, ch),
        bias_first.reshape(1, -1),
        conv_second.reshape(3, 3 * ch, ch),
        sounding_tile.T,
        sounding_cells.T,
        cell_weights.T,
        observations.T,
        layer_in,
        bias_in.reshape(1, -1),
        layer_out.T,
        bias_out,
        error_precision,
    ))
    return pl.pallas_call(
        functools.partial(kernel, n),
        out_shape=jax.ShapeDtypeStruct(state.shape, F32),
        in_specs=[pl.BlockSpec(memory_space=pltpu.SMEM)] + [hbm] * len(operands),
        out_specs=vmem,
        scratch_shapes=[pltpu.VMEM(x.shape, x.dtype) for x in operands]
        + [pltpu.VMEM((12 * ch, 2 * ch), BF16)] * 4
        + [
            pltpu.VMEM((listed, chan), F32),
            pltpu.VMEM((chan, hid), BF16),
            pltpu.VMEM((2, rows, cols, ch), BF16),
            pltpu.VMEM((2, 2, 2, cols, ch), BF16),
            pltpu.VMEM((cols, (rows + 4) * 3 * ch), BF16),
            pltpu.VMEM((rows + 2, cols, ch), F32),
            pltpu.VMEM((cols, (rows + 2) * 3 * ch), BF16),
            pltpu.VMEM((cols, ch), F32),
            pltpu.VMEM((cols, ch), F32),
            pltpu.VMEM((slots // LANES, 2 * margin, LANES), F32),
            pltpu.VMEM((slots // LANES, 2 * margin, LANES), F32),
            pltpu.VMEM((ch, rows * cols), BF16),
            pltpu.VMEM((2 * margin, listed), F32),
            pltpu.VMEM((listed, slots), BF16),
            pltpu.VMEM((slots, listed), BF16),
            pltpu.VMEM((rows * cols, slots), BF16),
            pltpu.VMEM((listed, ch), BF16),
            pltpu.VMEM((n, 1, max(2 * margin * cap, LANES)), F32),
            pltpu.VMEM((n, 1, max(2 * margin * cap, LANES)), F32),
            pltpu.VMEM((n, cap, ch), BF16),
            pltpu.VMEM((n, cap, ch), BF16),
            pltpu.VMEM((n, cap, ch), BF16),
            pltpu.VMEM((n, cap, ch), BF16),
            dma((len(operands),)),
            dma((2, 2, 2)),
            dma((2, 2, 2)),
            dma,
            dma,
            dma,
            dma,
            dma,
            dma,
        ],
        compiler_params=pltpu.CompilerParams(
            collective_id=0, has_side_effects=True, vmem_limit_bytes=48 * 1024 * 1024
        ),
        name="step",
    )(live_counts, *operands)


def solution(mesh):
    split = P("dev")
    return jax.shard_map(
        per_device,
        mesh=mesh,
        in_specs=(
            split, split, P(), P(), P(), P(), split, split, split, split, split, P(), P(), P(), P(), P(),
        ),
        out_specs=split,
        check_vma=False,
    )
```

time: 54 us -> 46.3 us (0.86)
  Pallas kernels: 52.2 us -> 44.5 us
    pallas_call x1, Pallas kernels: 52.2 us -> 44.5 us  [per_device(): pl.pallas_call(functools.partial(kernel, n), out_shape=jax.ShapeDtypeStru...]
where the time goes in v2:
time: 46.3 us; the launch traced here: 46.1 us
  Pallas kernels  44.5 us (96%)
  local copies, waits for them, and re-layouts  0.97 us (2%)
  between operations  0.66 us (1%)
    pallas_call x1, Pallas kernels, per_device(): pl.pallas_call(functools.partial(kernel, n), out_shape=jax.ShapeDtypeStru...  44.5 us
    unnamed x1, local copies, waits for them, and re-layouts  0.97 us

profile of v2, /device:TPU:1, one launch (start us, length us, event | category | flops | bytes accessed | tf_op | source)
XLA Modules:
  0.0 46.1 jit_solution(1412423620463632125)
XLA Ops:
  0.7 44.5 %step.1 = f32[4,512,128]{2,1,0:T(8,128)S(1)} custom-call(s32[1]{0:T(128)S(6)} %copy.18.live_ref, f32[4,512,128]{2,1,0:T(8,128)} %state_hbm.1, f32[4,512,128]{2,1,0:T(8,128)} %background_hbm.1, f32[1,128]{1,0:T(1,128)} %bitcast.18, bf16[3,384,128]{2,1,0:T(8,128)(2,1)} %bitcast.12, f32[1,128]{1,0:T(1,128)} %bitcast.19, bf16[3,384,128]{2,1,0:T(8,128)(2,1)} %bitcast.13, ...), custom_call_target="tpu_custom_call" | custom-call | tf_op jit(solution)/shard_map/step/pallas_call | solution.py:571
  45.1 1.0 %copy.19 = f32[4,512,128]{2,1,0:T(8,128)} copy(f32[4,512,128]{2,1,0:T(8,128)S(1)} %step.1) | data formatting | bytes 2097152

commit v3 on v2

--- a/solution.py
+++ b/solution.py
@@ -70,6 +70,8 @@
     edge_ref,
     local_ref,
     share_ref,
+    near_ref,
+    gathered_ref,
     observed_t_ref,
     values_ref,
     place_ref,
@@ -154,33 +156,53 @@
     for load in loads[4:]:
         load.start()
 
+    outer = ((my_quarter == 0) | (my_quarter == 3)).astype(jnp.int32)
+
     def by_quarters(fill, serve):
         sub = lax.rem(my_quarter, 2)
+        far_a = (1 - my_half) * 2 + sub
+        far_b = (1 - my_half) * 2 + 1 - sub
+        beside = my_half * 2 + 1 - sub
+        first = ((far_a, far_a), (far_b, beside), (beside, far_b), (my_quarter, my_quarter))
+        is_near = ((0, 0), (0, 1), (1, 0), (1, 1))
         for step in range(4):
-            which = (my_half if step > 1 else 1 - my_half) * 2 + lax.rem(sub + (step + step // 2) % 2, 2)
+            which = first[step][0] * (1 - outer) + first[step][1] * outer
+            near = is_near[step][0] * (1 - outer) + is_near[step][1] * outer
             fill(which)
 
             def one(j, carry):
-                serve(which * quarter + lax.rem(me + j, quarter))
+                serve(which * quarter + lax.rem(me + j, quarter), near)
                 return carry
 
             lax.fori_loop(1 if step == 3 else 0, quarter, one, 0)
 
+    def by_halves(fill, serve):
+        for step in range(2):
+            near = step
+            which = my_half if near else 1 - my_half
+            fill(which)
+
+            def one(j, carry):
+                serve(which * half + lax.rem(me + j + near, half), near)
+                return carry
+
+            lax.fori_loop(0, half - near, one, 0)
+
     def post(src, dst, send, recv):
-        def one(target):
+        def one(target, near=None):
             pltpu.make_async_remote_copy(
                 src_ref=src.at[target],
                 dst_ref=dst.at[me],
                 send_sem=send,
-                recv_sem=recv,
+                recv_sem=recv if near is None else recv.at[near],
                 device_id=(target,),
                 device_id_type=MESH,
             ).start()
 
         return one
 
-    def settle(dst, sem):
-        blocks = dst.at[pl.ds(0, n - 1)]
+    def settle(dst, sem, count):
+        blocks = dst.at[pl.ds(0, count)]
         pltpu.make_async_copy(blocks, blocks, sem).wait()
 
     def rim(phase, side, depth):
@@ -194,19 +216,15 @@
             device_id_type=MESH,
         )
 
-    sends = (me < n - 1, me > 0)
-
-    def rim_start(phase, depth):
-        for side in range(2):
-
-            @pl.when(sends[side])
-            def _():
-                rim(phase, side, depth).start()
+    def rim_start(phase, side, depth):
+        @pl.when(((side == 0) & (me < n - 1)) | ((side == 1) & (me > 0)))
+        def _():
+            rim(phase, side, depth).start()
 
     def rim_sent(phase, depth):
         for side in range(2):
 
-            @pl.when(sends[side])
+            @pl.when(me < n - 1 if side == 0 else me > 0)
             def _():
                 rim(phase, side, depth).wait_send()
 
@@ -351,8 +369,9 @@
     pl.semaphore_wait(barrier, n - 1)
     far_half(post(req_src, req_dst, req_send, req_recv))
     near_half(post(req_src, req_dst, req_send, req_recv))
-    rim_start(0, 0)
-    rim_start(0, 1)
+    for side in (close, 1 - close):
+        for depth in range(2):
+            rim_start(0, side, depth)
 
     loads[4].wait()
     loads[5].wait()
@@ -362,7 +381,7 @@
 
     conv_inside(*forward)
     conv_side(close, 0, *forward)
-    settle(req_dst, req_recv)
+    settle(req_dst, req_recv, n - 1)
     for g in range(groups):
         sent = []
         for i in range(per):
@@ -389,36 +408,35 @@
         cell = cell.astype(F32).astype(BF16)
 
         def spread_row(row):
-            return jnp.broadcast_to(row, (16, LANES)).astype(BF16)[None]
+            return jnp.broadcast_to(row, (16, LANES)).astype(BF16)
 
         local = local_ref[g]
-        share = share_ref[g][0:margin]
+        share = share_ref[g]
+        chunk = [spread_row(local[margin + k : margin + k + 1]) for k in range(margin)]
+        weight = [spread_row(share[k : k + 1]) for k in range(margin)]
         hit = [
-            jnp.where(cell == spread_row(local[k : k + 1]), 1.0, 0.0).astype(BF16)
+            jnp.where(cell == spread_row(local[k : k + 1])[None], 1.0, 0.0).astype(BF16)
             for k in range(margin)
         ]
         for c in range(rows * cols // LANES):
-            here = jnp.where(local[margin:] == c, share, 0.0)
-            total = hit[0] * spread_row(here[0:1])
-            for k in range(1, margin):
-                total = total + hit[k] * spread_row(here[k : k + 1])
+            total = None
+            for k in range(margin):
+                here = jnp.where(chunk[k] == c, weight[k], jnp.zeros_like(weight[k]))
+                term = hit[k] * here[None]
+                total = term if total is None else total + term
             share_t_ref[pl.ds(c * LANES, LANES), at(g * LANES, LANES)] = total.reshape(LANES, LANES)
         return carry
 
     lax.fori_loop(0, groups, build_shares, 0)
     conv_side(1 - close, 0, *forward)
 
-    ret = post(ret_src, ret_dst, ret_send, ret_recv)
 
     def blend(which):
         base = which * (slots // 2)
         blended = dot(observed_t_ref[...], share_t_ref[:, at(base, slots // 2)]).T
         ret_src[pl.ds(which * half, half)] = blended.reshape(half, cap, ch).astype(BF16)
 
-    blend(1 - my_half)
-    far_half(ret)
-    blend(my_half)
-    near_half(ret)
+    by_halves(blend, post(ret_src, ret_dst, ret_send, ret_recv))
     ret_dst[me] = ret_src[me]
 
     rank_col = jnp.sum(jnp.where(same & (from_row < from_col), 1.0, 0.0), axis=1, keepdims=True)
@@ -454,18 +472,24 @@
             dot(high, layer_out_ref[...]) + dot(low, layer_out_ref[...])
         ).astype(BF16)
 
-    def flat(ref):
+    def flat(ref, which):
+        blocks = ref[pl.ds(which * half, half)]
         if cap % 16 == 0:
-            return ref[...].reshape(slots, ch)
-        return ref[...].astype(F32).reshape(slots, ch).astype(BF16)
-
-    settle(ret_dst, ret_recv)
-    returned = flat(ret_dst)
+            return blocks.reshape(half * cap, ch)
+        return blocks.astype(F32).reshape(half * cap, ch).astype(BF16)
+
+    near_lanes = at(my_half * (slots // 2), slots // 2)
+    far_lanes = at((1 - my_half) * (slots // 2), slots // 2)
+
+    settle(ret_dst, ret_recv.at[1], half - 1)
+    near_ref[...] = dot(place_ref[:, near_lanes], flat(ret_dst, my_half))
+    settle(ret_dst, ret_recv.at[0], half)
+    returned = flat(ret_dst, 1 - my_half)
     live = live_ref[0]
     block = listed // 2
     for s in range(0, listed, block):
         span = pl.ds(s, block)
-        interpolated = dot(place_ref[span], returned).astype(BF16)
+        interpolated = (near_ref[span] + dot(place_ref[span, far_lanes], returned)).astype(BF16)
         activated = jnp.tanh(dot(interpolated, layer_in_ref[...]) + bias_in_ref[...]).astype(BF16)
         innovation = dot_nt(activated, layer_out_ref[...]) + offset_ref[span]
         alive = lax.broadcasted_iota(jnp.int32, (block, 1), 0) + s < live
@@ -475,31 +499,34 @@
         pre_grad = (back_act * (1.0 - act_wide * act_wide)).astype(BF16)
         grad_ref[span] = dot_nt(pre_grad, layer_in_ref[...]).astype(BF16)
 
-    out = post(out_src, out_dst, out_send, out_recv)
 
     def dispatch(which):
         base = which * (slots // 4)
         outgoing = dot(place_t_ref[at(base, slots // 4)], grad_ref[...])
         out_src[pl.ds(which * quarter, quarter)] = outgoing.reshape(quarter, cap, ch).astype(BF16)
 
-    by_quarters(dispatch, out)
+    by_quarters(dispatch, post(out_src, out_dst, out_send, out_recv))
     out_dst[me] = out_src[me]
-    settle(out_dst, out_recv)
-    arrived = flat(out_dst)
+    settle(out_dst, out_recv.at[1], half - 1)
+    arrived = flat(out_dst, my_half)
+    for r in range(rows):
+        gathered_ref[r] = dot(share_t_ref[pl.ds(r * cols, cols), near_lanes], arrived)
+    settle(out_dst, out_recv.at[0], half)
 
     def gather_grad(r):
-        value = dot(share_t_ref[pl.ds(r * cols, cols)], arrived)
+        arrived = flat(out_dst, 1 - my_half)
+        value = gathered_ref[r] + dot(share_t_ref[at(r * cols, cols), far_lanes], arrived)
+        field_ref[1, r] = value.astype(BF16)
         out_ref[r] = out_ref[r] + value
-        value = value.astype(BF16)
-        field_ref[1, r] = value
-        put_taps(taps_ref, r + 2, value.astype(F32))
-
-    gather_grad(0)
-    gather_grad(rows - 1)
-    rim_start(1, 0)
-    for r in range(1, rows - 1):
+
+    for side in (close, 1 - close):
+        for depth in range(2):
+            gather_grad((1 - side) * (rows - 1 - depth) + side * depth)
+            rim_start(1, side, depth)
+    for r in range(2, rows - 2):
         gather_grad(r)
-    rim_start(1, 1)
+    for r in range(rows):
+        put_taps(taps_ref, r + 2, field_ref[1, r].astype(F32))
 
     def put_act(slot, value, keep=None):
         hidden = hidden_ref[slot]
@@ -518,9 +545,9 @@
     for phase in range(2):
         for depth in range(2):
             rim_sent(phase, depth)
-    settle(req_src, req_send)
-    settle(ret_src, ret_send)
-    settle(out_src, out_send)
+    settle(req_src, req_send, n - 1)
+    settle(ret_src, ret_send, n - 1)
+    settle(out_src, out_send, n - 1)
 
 
 def per_device(
@@ -587,6 +614,8 @@
             pltpu.VMEM((cols, ch), F32),
             pltpu.VMEM((slots // LANES, 2 * margin, LANES), F32),
             pltpu.VMEM((slots // LANES, 2 * margin, LANES), F32),
+            pltpu.VMEM((listed, ch), F32),
+            pltpu.VMEM(state.shape, F32),
             pltpu.VMEM((ch, rows * cols), BF16),
             pltpu.VMEM((2 * margin, listed), F32),
             pltpu.VMEM((listed, slots), BF16),
@@ -605,9 +634,9 @@
             dma,
             dma,
             dma,
+            dma((2,)),
             dma,
-            dma,
-            dma,
+            dma((2,)),
         ],
         compiler_params=pltpu.CompilerParams(
             collective_id=0, has_side_effects=True, vmem_limit_bytes=48 * 1024 * 1024

time: 46.3 us -> 45.4 us (0.981)
  Pallas kernels: 44.5 us -> 43.6 us
    pallas_call x1, Pallas kernels: 44.5 us -> 43.6 us  [per_device(): pl.pallas_call(functools.partial(kernel, n), out_shape=jax.ShapeDtypeStru...]
where the time goes in v3:
time: 45.4 us; the launch traced here: 45.3 us
  Pallas kernels  43.6 us (96%)
  local copies, waits for them, and re-layouts  0.97 us (2%)
  between operations  0.66 us (1%)
    pallas_call x1, Pallas kernels, per_device(): pl.pallas_call(functools.partial(kernel, n), out_shape=jax.ShapeDtypeStru...  43.6 us
    unnamed x1, local copies, waits for them, and re-layouts  0.97 us

profile of v3, /device:TPU:1, one launch (start us, length us, event | category | flops | bytes accessed | tf_op | source)
XLA Modules:
  0.0 45.3 jit_solution(9226183508666106052)
XLA Ops:
  0.7 43.6 %step.1 = f32[4,512,128]{2,1,0:T(8,128)S(1)} custom-call(s32[1]{0:T(128)S(6)} %copy.18.live_ref, f32[4,512,128]{2,1,0:T(8,128)} %state_hbm.1, f32[4,512,128]{2,1,0:T(8,128)} %background_hbm.1, f32[1,128]{1,0:T(1,128)} %bitcast.18, bf16[3,384,128]{2,1,0:T(8,128)(2,1)} %bitcast.12, f32[1,128]{1,0:T(1,128)} %bitcast.19, bf16[3,384,128]{2,1,0:T(8,128)(2,1)} %bitcast.13, ...), custom_call_target="tpu_custom_call" | custom-call | tf_op jit(solution)/shard_map/step/pallas_call | solution.py:598
  44.3 1.0 %copy.19 = f32[4,512,128]{2,1,0:T(8,128)} copy(f32[4,512,128]{2,1,0:T(8,128)S(1)} %step.1) | data formatting | bytes 2097152
